TPU v7x, 32 devices: a whole 2x2x4 slice. The times are simulated.
32 devices in a mesh: seq: 8 (over z, y), head: 4 (over x, core).
Axes of the slice: x: 2, y: 2, z: 4, core: 2. Of those that a mesh axis runs over, the one named last changes fastest.
Arguments:
- queries: bfloat16 [1024, 4096], P('seq', 'head'), may hold values from -40 to 40
- keys: bfloat16 [1024, 512], P(('seq', 'head')), may hold values from -40 to 40
- values: bfloat16 [1024, 512], P(('seq', 'head')), may hold values from -6 to 6
- block_order: int32 [8], replicated, may hold values from 0 to 7, each once
Outputs:
- attended: bfloat16 [1024, 4096], P('seq', 'head')
All inputs are finite; a program needn't handle non-finite values.
Results may differ from a plain program's by a relative error of at most 0.0055.
Values may be sent and summed in bfloat16 or wider, within the bound.
A program may use at most 64 MiB of HBM per device.

v0:
```python
import math

import jax
import jax.numpy as jnp
from jax import lax
from jax.sharding import PartitionSpec as P

HD = 128
GROUP = 8


def local(queries, keys, values, block_order):
    key_rows, value_rows = (
        lax.all_to_all(keys, "head", split_axis=1, concat_axis=0, tiled=True),
        lax.all_to_all(values, "head", split_axis=1, concat_axis=0, tiled=True),
    )
    block_len = queries.shape[0]
    kv_local = key_rows.shape[1] // HD
    devices = lax.axis_size("seq")
    query_heads = queries.reshape(block_len, kv_local, GROUP, HD)
    mine = block_order[lax.axis_index("seq")]
    query_pos = mine * block_len + jnp.arange(block_len, dtype=jnp.int32)
    factor = 1.0 / math.sqrt(HD)
    start_state = (
        jnp.full((kv_local, GROUP, block_len), -1e30, jnp.float32),
        jnp.zeros((kv_local, GROUP, block_len), jnp.float32),
        jnp.zeros((block_len, kv_local, GROUP, HD), jnp.float32),
    )

    def absorb(state, key_block, value_block, key_pos):
        highest, totals, running = state
        count_rows = key_block.shape[0]
        key_cols = key_block.reshape(count_rows, kv_local, HD)
        value_cols = value_block.reshape(count_rows, kv_local, HD)
        scores = (
            jnp.einsum("qhgd,khd->hgqk", query_heads, key_cols, preferred_element_type=jnp.float32)
            * factor
        )
        visible = query_pos[:, None] >= key_pos[None, :]
        scores = jnp.where(visible, scores, -1e30)
        new_high = jnp.maximum(highest, jnp.max(scores, axis=-1))
        weights = jnp.where(visible, jnp.exp(scores - new_high[..., None]), 0.0)
        rescale = jnp.exp(highest - new_high)
        totals = totals * rescale + jnp.sum(weights, axis=-1)
        product = jnp.einsum(
            "hgqk,khd->qhgd",
            weights.astype(jnp.bfloat16),
            value_cols,
            preferred_element_type=jnp.float32,
        )
        running = running * jnp.transpose(rescale, (2, 0, 1))[..., None] + product
        return (new_high, totals, running)

    every_key, every_value = (
        lax.all_gather(key_rows, "seq", axis=0, tiled=True),
        lax.all_gather(value_rows, "seq", axis=0, tiled=True),
    )
    device_ids = jnp.arange(devices, dtype=jnp.int32)
    owner_of = jnp.sum(
        jnp.where(block_order[None, :] == device_ids[:, None], device_ids[None, :], 0), axis=1
    )
    sorted_keys = jnp.take(every_key.reshape(devices, block_len, -1), owner_of, axis=0).reshape(
        devices * block_len, -1
    )
    sorted_values = jnp.take(every_value.reshape(devices, block_len, -1), owner_of, axis=0).reshape(
        devices * block_len, -1
    )
    width = min(1024, devices * block_len)
    needed = ((mine + 1) * block_len + width - 1) // width

    def visit(number, state):
        first = (number * width).astype(jnp.int32)
        key_block = lax.dynamic_slice_in_dim(sorted_keys, first, width, 0)
        value_block = lax.dynamic_slice_in_dim(sorted_values, first, width, 0)
        key_pos = first + jnp.arange(width, dtype=jnp.int32)
        return absorb(state, key_block, value_block, key_pos)

    final_state = lax.fori_loop(0, needed, visit, start_state)
    highest, totals, running = final_state
    output = running / jnp.transpose(totals, (2, 0, 1))[..., None]
    return output.reshape(block_len, kv_local * GROUP * HD).astype(jnp.bfloat16)


def solution(mesh):
    placed = (P("seq", "head"), P(("seq", "head"), None), P(("seq", "head"), None), P())
    return jax.shard_map(
        local, mesh=mesh, in_specs=placed, out_specs=P("seq", "head"), check_vma=False
    )
```

profile of v0, /device:TPU:0, one launch (start us, length us, event | category | flops | bytes accessed | tf_op | source)
XLA Modules:
  0.0 83.4 jit_solution(11807065561781703888)
XLA Ops:
  0.0 0.0 copy-start
  0.0 0.8 copy-done
  0.8 0.6 copy_bitcast_fusion.2
  1.4 4.2 %all-to-all-start = ((bf16[32,4,128]{2,0,1:T(8,128)(2,1)}), bf16[32,4,128]{2,0,1:T(8,128)(2,1)S(1)}, u32[]{:S(2)}, u32[]{:S(2)}) async-start(bf16[32,4,128]{2,0,1:T(8,128)(2,1)} %copy_bitcast_fusion.2), calls=%async_computation | async-start | bytes 65536 | tf_op jit(solution)/shard_map/all_to_all | solution.py:14
  5.6 0.8 select_reduce_fusion
  6.4 1.4 %copy_bitcast_fusion.1 = bf16[32,4,128]{2,0,1:T(8,128)(2,1)} fusion(bf16[32,512]{1,0:T(8,128)(2,1)} %param.10), kind=kLoop, calls=%fused_computation.31 | loop fusion | bytes 65536 | tf_op jit(solution)/shard_map/all_to_all | solution.py:15
  7.8 1.2 %dynamic_slice.2 = s32[1]{0:T(128)} dynamic-slice(s32[8]{0:T(128)} %param.11, s32[]{:T(128)S(6)} %select_n.28), dynamic_slice_sizes={1} | dynamic-slice | bytes 12 | tf_op jit(solution)/shard_map/dynamic_slice | solution.py:21
  10.3 1.1 %copy.24 = bf16[128,1024]{0,1:T(8,128)(2,1)S(1)} copy(bf16[128,1024]{1,0:T(8,128)(2,1)} %param.8) | data formatting | bytes 524288 | tf_op args[0]
  11.4 0.2 copy.27
  11.6 0.0 all-to-all-done
  11.6 3.3 %all-to-all-start.1 = ((bf16[32,4,128]{2,0,1:T(8,128)(2,1)}), bf16[32,4,128]{2,0,1:T(8,128)(2,1)S(1)}, u32[]{:S(2)}, u32[]{:S(2)}) async-start(bf16[32,4,128]{2,0,1:T(8,128)(2,1)} %copy_bitcast_fusion.1), calls=%async_computation.1 | async-start | bytes 65536 | tf_op jit(solution)/shard_map/all_to_all | solution.py:15
  14.9 31.7 %all_gather.6 = bf16[1024,128]{1,0:T(8,128)(2,1)S(1)} all-gather(bf16[128,128]{1,0:T(8,128)(2,1)S(1)} %bitcast.120), channel_id=1, replica_groups=mesh['seq'=8,'head'=4] {'seq'}, dimensions={0}, use_global_device_ids=true | all-gather | bytes 294912 | tf_op jit(solution)/shard_map/all_gather | solution.py:55
  46.6 0.0 all-to-all-done.1
  46.6 30.7 %all_gather.7 = bf16[1024,128]{1,0:T(8,128)(2,1)S(1)} all-gather(bf16[128,128]{1,0:T(8,128)(2,1)S(1)} %bitcast.121), channel_id=1, replica_groups=mesh['seq'=8,'head'=4] {'seq'}, dimensions={0}, use_global_device_ids=true | all-gather | bytes 294912 | tf_op jit(solution)/shard_map/all_gather | solution.py:56
  77.3 0.6 gather_fusion
  77.9 0.6 gather_fusion.1
  78.6 0.1 broadcast_select_fusion
  78.7 3.5 %while.15 = (s32[]{:T(128)}, f32[1,8,128]{2,1,0:T(8,128)S(1)}, f32[1,8,128]{2,1,0:T(8,128)S(1)}, f32[128,1,8,128]{3,0,2,1:T(8,128)S(1)}, s32[]{:T(128)}, /*index...) while((s32[]{:T(128)}, f32[1,8,128]{2,1,0:T(8,128)S(1)}, ...), condition=%wide.region_4.6_spmd.clone, body=%wide.region_1.5_spmd.clone.sunk | while | flops 550899840 | bytes 15017089 | solution.py:78
  78.8 0.2 broadcast_compare_fusion.2
  79.0 0.8 fusion.33
  79.8 1.4 %fusion.36 = f32[128,1,8,128]{3,0,2,1:T(8,128)S(1)} fusion(f32[1024,128,8]{1,0,2:T(8,128)S(1)} %get-tuple-element.201, f32[8,128]{1,0:T(8,128)S(1)} %bitcast.112, pred[128,1024]{0,1:T(8,128)(4,1)S(1)} %broadcast_compare_fusion.2, f32[128,1,8,128]{3,0,2,1:T(8,128)S(1)} %get-tuple-element.217, bf16[1024,128]{1,0:T(8,128)(2,1)S(1)} %get-tuple-element.232, ...), kind=kOutput, calls=%fused_computation.12.clone.1 | convolution fusion | flops 273940480 | bytes 5644288 | tf_op jit(solution)/shard_map/while/body/hgqk,khd->qhgd/dot_general | solution.py:45
  81.2 1.0 %fusion.35 = f32[8,128]{1,0:T(8,128)S(1)} fusion(f32[1024,128,8]{1,0,2:T(8,128)S(1)} %get-tuple-element.201, f32[8,128]{1,0:T(8,128)S(1)} %bitcast.113, pred[128,1024]{0,1:T(8,128)(4,1)S(1)} %broadcast_compare_fusion.2), kind=kLoop, calls=%fused_computation.7.clone.1 | loop fusion | flops 5241856 | bytes 4333568 | tf_op jit(solution)/shard_map/while/body/reduce_sum | solution.py:44
  82.3 0.2 divide_convert_fusion
  82.5 0.2 copy.28
  82.7 0.8 copy.36
  (11 shorter events, 0.1 us)
Async XLA Ops:
  0.0 0.8 copy-start
  1.4 10.2 %all-to-all-start = ((bf16[32,4,128]{2,0,1:T(8,128)(2,1)}), bf16[32,4,128]{2,0,1:T(8,128)(2,1)S(1)}, u32[]{:S(2)}, u32[]{:S(2)}) async-start(bf16[32,4,128]{2,0,1:T(8,128)(2,1)} %copy_bitcast_fusion.2), calls=%async_computation | async-start | bytes 65536 | tf_op jit(solution)/shard_map/all_to_all | solution.py:14
  11.6 35.0 %all-to-all-start.1 = ((bf16[32,4,128]{2,0,1:T(8,128)(2,1)}), bf16[32,4,128]{2,0,1:T(8,128)(2,1)S(1)}, u32[]{:S(2)}, u32[]{:S(2)}) async-start(bf16[32,4,128]{2,0,1:T(8,128)(2,1)} %copy_bitcast_fusion.1), calls=%async_computation.1 | async-start | bytes 65536 | tf_op jit(solution)/shard_map/all_to_all | solution.py:15
where the time goes:
time: 83.9 us; the launch traced here: 83.4 us
  blocking collectives  62.4 us (74%)
  starting transfers between devices  7.54 us (9%)
  local copies, waits for them, and re-layouts  7.47 us (9%)
  other arithmetic  2.35 us (3%)
  matrix products  2.18 us (3%)
  between operations  1.37 us (2%)
    all_gather x1, blocking collectives, local(): lax.all_gather(key_rows, 'seq', axis=0, tiled=True)  31.7 us
    all_gather x1, blocking collectives, local(): lax.all_gather(value_rows, 'seq', axis=0, tiled=True)  30.7 us
    all_to_all x1, starting transfers between devices, local(): lax.all_to_all(keys, 'head', split_axis=1, concat_axis=0, tiled=True)  4.24 us
    all_to_all x1, starting transfers between devices, local(): lax.all_to_all(values, 'head', split_axis=1, concat_axis=0, tiled=True)  3.3 us
    unnamed x5, local copies, waits for them, and re-layouts  2.81 us
  transfers between devices with their start and end apart: 2, of which 0 were waited for; matrix products, arithmetic and copies ran while one was open for 6% of the time, Pallas kernels for 0%

commit v1 on v0

v1 whole, which is shorter than its diff:
```python
import functools
import math

import jax
import jax.numpy as jnp
from jax import lax
from jax.experimental import pallas as pl
from jax.experimental.pallas import tpu as pltpu
from jax.sharding import PartitionSpec as P

HD = 128
NEG = -1e30
MESH = pl.DeviceIdType.MESH


def kernel(
    outer, inner, heads,
    order, q_hbm, k_hbm, v_hbm, out_ref,
    q_ref, k_ref, v_ref, kz, vz, kd, vd, acc, high, total,
    load_sem, zsend, zrecv, psend, precv,
):
    rows, _ = k_ref.shape
    block = q_ref.shape[0]
    width = kd.shape[-1]
    q_heads = q_ref.shape[1] // HD
    seq, head = lax.axis_index("seq"), lax.axis_index("head")
    o, j = seq // inner, lax.rem(seq, inner)
    power = outer & (outer - 1) == 0

    def source(k):
        return jnp.bitwise_xor(o, k) if power else lax.rem(o - k + outer, outer)

    def target(k):
        return jnp.bitwise_xor(o, k) if power else lax.rem(o + k, outer)

    loads = [
        pltpu.make_async_copy(src, dst, load_sem.at[i])
        for i, (src, dst) in enumerate(((k_hbm, k_ref), (v_hbm, v_ref), (q_hbm, q_ref)))
    ]
    for load in loads:
        load.start()

    group = [(dj, dh) for dj in range(inner) for dh in range(heads)]

    def member(dj, dh):
        return lax.rem(j + dj, inner), lax.rem(head + dh, heads)

    barrier = pltpu.get_barrier_semaphore()
    for dj, dh in group[1:]:
        j2, h2 = member(dj, dh)
        pl.semaphore_signal(barrier, inc=1, device_id=(o * inner + j2, h2), device_id_type=MESH)

    def greet(k, c):
        pl.semaphore_signal(
            barrier, inc=1, device_id=(target(k) * inner + j, head), device_id_type=MESH
        )
        return c

    def steps(first, last, body):
        if last - first <= 8:
            for k in range(first, last):
                body(k, 0)
        else:
            lax.fori_loop(first, last, body, 0)

    steps(1, outer, greet)
    pl.semaphore_wait(barrier, len(group) - 1 + outer - 1)
    loads[0].wait()
    loads[1].wait()

    def zcopy(k, which):
        own, far = ((k_ref, kz), (v_ref, vz))[which]
        return pltpu.make_async_remote_copy(
            src_ref=own,
            dst_ref=far.at[k - 1],
            send_sem=zsend.at[which],
            recv_sem=zrecv.at[k, which],
            device_id=(target(k) * inner + j, head),
            device_id_type=MESH,
        )

    def scatter(piece, k, which):
        dst = (kd, vd)[which]
        place = pl.ds(pl.multiple_of(j * block + head * rows, rows), rows)
        for dj, dh in group:
            j2, h2 = member(dj, dh)
            src = piece.at[:, pl.ds(pl.multiple_of(h2 * width, width), width)]
            if dj == 0 and dh == 0:
                pltpu.make_async_copy(src, dst.at[k, place], load_sem.at[3 + which]).start()
            else:
                pltpu.make_async_remote_copy(
                    src_ref=src,
                    dst_ref=dst.at[k, place],
                    send_sem=psend.at[k, which],
                    recv_sem=precv.at[k, which],
                    device_id=(o * inner + j2, h2),
                    device_id_type=MESH,
                ).start()
        src = piece.at[:, pl.ds(pl.multiple_of(head * width, width), width)]
        pltpu.make_async_copy(src, dst.at[k, place], load_sem.at[3 + which]).wait()

    others = pl.ds(0, (len(group) - 1) * rows)

    def landed(k, which):
        dst = (kd, vd)[which].at[k, others]
        pltpu.make_async_copy(dst, dst, precv.at[k, which]).wait()

    def relay(k, c=0):
        for which in range(2):
            zcopy(k, which).wait_recv()
            scatter((kz, vz)[which].at[k - 1], k, which)
        return c

    mine = order[seq]
    factor = math.log2(math.e) / math.sqrt(HD)
    per = 2 if q_heads % 2 == 0 else 1
    lanes = per * block
    count = inner * block

    def absorb(k, first):
        src = source(k) * inner
        row = lax.broadcasted_iota(jnp.int32, (count, lanes), 0)
        col = lax.broadcasted_iota(jnp.int32, (count, lanes), 1)
        start = jnp.full((count, lanes), order[src], jnp.int32) * block
        for jj in range(1, inner):
            start = jnp.where(row >= jj * block, order[src + jj] * block - jj * block, start)
        visible = mine * block + lax.rem(col, block) >= start + row
        landed(k, 0)
        key = kd[k]
        for c in range(q_heads // per):
            q = jnp.concatenate(
                [q_ref[:, (c * per + i) * HD : (c * per + i + 1) * HD] for i in range(per)], axis=0
            )
            s = lax.dot_general(
                key, q, (((1,), (1,)), ((), ())), preferred_element_type=jnp.float32
            )
            s = jnp.where(visible, s * factor, NEG)
            at = slice(c * lanes, (c + 1) * lanes)
            top = jnp.max(s, axis=0, keepdims=True)
            if not first:
                old = high[:, at]
                top = jnp.maximum(old, top)
            p = jnp.exp2(s - top)
            high[:, at] = top
            t = jnp.sum(p, axis=0, keepdims=True)
            if c == 0:
                landed(k, 1)
                value = vd[k]
            pv = lax.dot_general(
                value,
                p.astype(jnp.bfloat16),
                (((0,), (0,)), ((), ())),
                preferred_element_type=jnp.float32,
            )
            if first:
                total[:, at] = t
                acc[:, at] = pv
            else:
                scale = jnp.exp2(old - top)
                total[:, at] = total[:, at] * scale + t
                acc[:, at] = acc[:, at] * scale + pv

    for which in range(2):
        steps(1, outer, lambda k, c, which=which: (zcopy(k, which).start(), c)[1])
        scatter((k_ref, v_ref)[which], 0, which)
    loads[2].wait()
    if outer > 1:
        relay(1)
    absorb(0, True)

    def later(k, c):
        relay(k + 1)
        absorb(k, False)
        return c

    steps(1, outer - 1, later)
    if outer > 1:
        absorb(outer - 1, False)

    for g in range(q_heads):
        at = slice(g * HD, (g + 1) * HD)
        lane = slice(g * block, (g + 1) * block)
        part = acc[:, lane] / total[:, lane]
        out_ref[:, at] = part.T.astype(out_ref.dtype)

    if outer > 1:
        for which in range(2):
            sent = (kz, vz)[which]
            pltpu.make_async_copy(sent, sent, zsend.at[which]).wait()

    def drain(k, c):
        for which in range(2):
            dst = (kd, vd)[which].at[k, others]
            pltpu.make_async_copy(dst, dst, psend.at[k, which]).wait()
        return c

    steps(0, outer, drain)


def local(devices, heads, queries, keys, values, block_order):
    inner = 2 if devices % 2 == 0 else 1
    outer = devices // inner
    rows, cols = keys.shape
    block, q_cols = queries.shape
    width = cols // heads
    assert width == HD and rows * heads == block
    bf16, f32 = jnp.bfloat16, jnp.float32
    far = max(outer - 1, 1)
    return pl.pallas_call(
        functools.partial(kernel, outer, inner, heads),
        out_shape=jax.ShapeDtypeStruct((block, q_cols), queries.dtype),
        in_specs=[pl.BlockSpec(memory_space=pltpu.SMEM)]
        + [pl.BlockSpec(memory_space=pl.ANY)] * 3,
        out_specs=pl.BlockSpec(memory_space=pltpu.VMEM),
        scratch_shapes=[
            pltpu.VMEM((block, q_cols), bf16),
            pltpu.VMEM((rows, cols), bf16),
            pltpu.VMEM((rows, cols), bf16),
            pltpu.VMEM((far, rows, cols), bf16),
            pltpu.VMEM((far, rows, cols), bf16),
            pltpu.VMEM((outer, inner * block, width), bf16),
            pltpu.VMEM((outer, inner * block, width), bf16),
            pltpu.VMEM((HD, q_cols // HD * block), f32),
            pltpu.VMEM((1, q_cols // HD * block), f32),
            pltpu.VMEM((1, q_cols // HD * block), f32),
            pltpu.SemaphoreType.DMA((5,)),
            pltpu.SemaphoreType.DMA((2,)),
            pltpu.SemaphoreType.DMA((outer, 2)),
            pltpu.SemaphoreType.DMA((outer, 2)),
            pltpu.SemaphoreType.DMA((outer, 2)),
        ],
        compiler_params=pltpu.CompilerParams(
            collective_id=0, has_side_effects=True, vmem_limit_bytes=48 * 1024 * 1024
        ),
    )(block_order, queries, keys, values)


def solution(mesh):
    placed = (P("seq", "head"), P(("seq", "head"), None), P(("seq", "head"), None), P())
    return jax.shard_map(
        functools.partial(local, mesh.shape["seq"], mesh.shape["head"]),
        mesh=mesh, in_specs=placed, out_specs=P("seq", "head"), check_vma=False,
    )
```

time: 83.9 us -> 23.5 us (0.28)
  blocking collectives: 62.4 us -> 0 us
  Pallas kernels: 0 us -> 19.4 us
  starting transfers between devices: 7.54 us -> 0 us
  local copies, waits for them, and re-layouts: 7.47 us -> 3.82 us
  other arithmetic: 2.35 us -> 0 us
  matrix products: 2.18 us -> 0 us
  between operations: 1.37 us -> 0.01 us
    all_gather x2 -> x0, blocking collectives: 62.4 us -> none  [the longest x1 31.7 us: local(): lax.all_gather(key_rows, 'seq', axis=0, tiled=True)]
    pallas_call x0 -> x1, Pallas kernels: none -> 19.4 us  [local(): pl.pallas_call(functools.partial(kernel, outer, inner, heads), out_shape=...]
    all_to_all x2 -> x0, starting transfers between devices: 7.54 us -> none  [the longest x1 4.24 us: local(): lax.all_to_all(keys, 'head', split_axis=1, concat_axis=0, tiled=True)]
    dot_general x2 -> x0, matrix products: 2.18 us -> none  [the longest x1 1.43 us: absorb(): jnp.einsum('hgqk,khd->qhgd', weights.astype(jnp.bfloat16), value_cols, pr...]
    all_to_all x2 -> x0, local copies, waits for them, and re-layouts: 2 us -> none  [the longest x1 1.38 us: local(): lax.all_to_all(values, 'head', split_axis=1, concat_axis=0, tiled=True)]
    reduce_sum x2 -> x0, other arithmetic: 1.78 us -> none  [the longest x1 1.01 us: absorb(): totals = totals * rescale + jnp.sum(weights, axis=-1)]
    dynamic_slice x1 -> x0, local copies, waits for them, and re-layouts: 1.25 us -> none  [local(): mine = block_order[lax.axis_index('seq')]]
    gather x2 -> x0, local copies, waits for them, and re-layouts: 1.19 us -> none  [the longest x1 0.6 us: local(): jnp.take(every_value.reshape(devices, block_len, -1), owner_of, axis=0)]
  transfers between devices with their start and end apart: 2 -> 0, of which waited for: 0 -> 0; matrix products, arithmetic and copies ran while one was open for 6% -> 0% of each run, Pallas kernels for 0% -> 0%
where the time goes in v1:
time: 23.5 us; the launch traced here: 23.3 us
  Pallas kernels  19.4 us (83%)
  local copies, waits for them, and re-layouts  3.82 us (16%)
    pallas_call x1, Pallas kernels, local(): pl.pallas_call(functools.partial(kernel, outer, inner, heads), out_shape=...  19.4 us
    unnamed x9, local copies, waits for them, and re-layouts  3.82 us

profile of v1, /device:TPU:0, one launch (start us, length us, event | category | flops | bytes accessed | tf_op | source)
XLA Modules:
  0.0 23.3 jit_solution(13522616752285108318)
XLA Ops:
  0.0 0.0 copy-start
  0.0 0.9 %copy-done = bf16[128,1024]{1,0:T(8,128)(2,1)S(1)} copy-done((bf16[128,1024]{1,0:T(8,128)(2,1)S(1)}, bf16[128,1024]{1,0:T(8,128)(2,1)}, u32[]{:S(2)}) %copy-start) | copy-done | bytes 262168
  1.0 0.0 copy-start.1
  1.0 0.8 %copy-done.1 = bf16[32,512]{1,0:T(8,128)(2,1)S(1)} copy-done((bf16[32,512]{1,0:T(8,128)(2,1)S(1)}, bf16[32,512]{1,0:T(8,128)(2,1)}, u32[]{:S(2)}) %copy-start.1) | copy-done | bytes 32792
  1.7 0.0 copy-start.2
  1.7 0.8 %copy-done.2 = bf16[32,512]{1,0:T(8,128)(2,1)S(1)} copy-done((bf16[32,512]{1,0:T(8,128)(2,1)S(1)}, bf16[32,512]{1,0:T(8,128)(2,1)}, u32[]{:S(2)}) %copy-start.2) | copy-done | bytes 32792
  2.5 0.0 copy-start.3
  2.5 0.7 %copy-done.3 = s32[8]{0:T(128)S(1)} copy-done((s32[8]{0:T(128)S(1)}, s32[8]{0:T(128)}, u32[]{:S(2)}) %copy-start.3) | copy-done | bytes 56
  3.1 19.4 %shard_map.46 = bf16[128,1024]{1,0:T(8,128)(2,1)S(1)} custom-call(s32[8]{0:T(128)S(1)} %copy-done.3, bf16[128,1024]{1,0:T(8,128)(2,1)S(1)} %copy-done, bf16[32,512]{1,0:T(8,128)(2,1)S(1)} %copy-done.1, bf16[32,512]{1,0:T(8,128)(2,1)S(1)} %copy-done.2), custom_call_target="tpu_custom_call" | custom-call | tf_op jit(solution)/shard_map/pallas_call | solution.py:209
  22.6 0.7 %copy.6 = bf16[128,1024]{1,0:T(8,128)(2,1)} copy(bf16[128,1024]{1,0:T(8,128)(2,1)S(1)} %shard_map.46) | data formatting | bytes 524288
Async XLA Ops:
  0.0 0.9 %copy-start = (bf16[128,1024]{1,0:T(8,128)(2,1)S(1)}, bf16[128,1024]{1,0:T(8,128)(2,1)}, u32[]{:S(2)}) copy-start(bf16[128,1024]{1,0:T(8,128)(2,1)} %q_hbm.1) | copy-start | bytes 786436
  1.0 0.8 %copy-start.1 = (bf16[32,512]{1,0:T(8,128)(2,1)S(1)}, bf16[32,512]{1,0:T(8,128)(2,1)}, u32[]{:S(2)}) copy-start(bf16[32,512]{1,0:T(8,128)(2,1)} %k_hbm.1) | copy-start | bytes 98308
  1.7 0.8 %copy-start.2 = (bf16[32,512]{1,0:T(8,128)(2,1)S(1)}, bf16[32,512]{1,0:T(8,128)(2,1)}, u32[]{:S(2)}) copy-start(bf16[32,512]{1,0:T(8,128)(2,1)} %v_hbm.1) | copy-start | bytes 98308
  2.5 0.7 %copy-start.3 = (s32[8]{0:T(128)S(1)}, s32[8]{0:T(128)}, u32[]{:S(2)}) copy-start(s32[8]{0:T(128)} %order.1) | copy-start | bytes 100

commit v2 on v1

--- a/solution.py
+++ b/solution.py
@@ -15,8 +15,8 @@
 
 def kernel(
     outer, inner, heads,
-    order, q_hbm, k_hbm, v_hbm, out_ref,
-    q_ref, k_ref, v_ref, kz, vz, kd, vd, acc, high, total,
+    order, q_hbm, k_hbm, v_hbm, acc, total,
+    q_ref, k_ref, v_ref, kz, vz, kd, vd, high,
     load_sem, zsend, zrecv, psend, precv,
 ):
     rows, _ = k_ref.shape
@@ -177,12 +177,6 @@
     if outer > 1:
         absorb(outer - 1, False)
 
-    for g in range(q_heads):
-        at = slice(g * HD, (g + 1) * HD)
-        lane = slice(g * block, (g + 1) * block)
-        part = acc[:, lane] / total[:, lane]
-        out_ref[:, at] = part.T.astype(out_ref.dtype)
-
     if outer > 1:
         for which in range(2):
             sent = (kz, vz)[which]
@@ -195,6 +189,14 @@
         return c
 
     steps(0, outer, drain)
+
+
+def finish(acc, total, out_ref):
+    block, q_cols = out_ref.shape
+    for g in range(q_cols // HD):
+        lane = slice(g * block, (g + 1) * block)
+        part = acc[:, lane] / total[:, lane]
+        out_ref[:, g * HD : (g + 1) * HD] = part.T.astype(out_ref.dtype)
 
 
 def local(devices, heads, queries, keys, values, block_order):
@@ -206,12 +208,16 @@
     assert width == HD and rows * heads == block
     bf16, f32 = jnp.bfloat16, jnp.float32
     far = max(outer - 1, 1)
-    return pl.pallas_call(
+    lanes = q_cols // HD * block
+    acc, total = pl.pallas_call(
         functools.partial(kernel, outer, inner, heads),
-        out_shape=jax.ShapeDtypeStruct((block, q_cols), queries.dtype),
+        out_shape=(
+            pltpu.VMEM((HD, lanes), f32),
+            pltpu.VMEM((1, lanes), f32),
+        ),
         in_specs=[pl.BlockSpec(memory_space=pltpu.SMEM)]
-        + [pl.BlockSpec(memory_space=pl.ANY)] * 3,
-        out_specs=pl.BlockSpec(memory_space=pltpu.VMEM),
+        + [pl.BlockSpec(memory_space=pltpu.HBM)] * 3,
+        out_specs=[pl.BlockSpec(memory_space=pltpu.VMEM)] * 2,
         scratch_shapes=[
             pltpu.VMEM((block, q_cols), bf16),
             pltpu.VMEM((rows, cols), bf16),
@@ -220,9 +226,7 @@
             pltpu.VMEM((far, rows, cols), bf16),
             pltpu.VMEM((outer, inner * block, width), bf16),
             pltpu.VMEM((outer, inner * block, width), bf16),
-            pltpu.VMEM((HD, q_cols // HD * block), f32),
-            pltpu.VMEM((1, q_cols // HD * block), f32),
-            pltpu.VMEM((1, q_cols // HD * block), f32),
+            pltpu.VMEM((1, lanes), f32),
             pltpu.SemaphoreType.DMA((5,)),
             pltpu.SemaphoreType.DMA((2,)),
             pltpu.SemaphoreType.DMA((outer, 2)),
@@ -230,9 +234,16 @@
             pltpu.SemaphoreType.DMA((outer, 2)),
         ],
         compiler_params=pltpu.CompilerParams(
-            collective_id=0, has_side_effects=True, vmem_limit_bytes=48 * 1024 * 1024
+            collective_id=0, has_side_effects=True, vmem_limit_bytes=67043328 - 600 * 1024
         ),
     )(block_order, queries, keys, values)
+    return pl.pallas_call(
+        finish,
+        out_shape=jax.ShapeDtypeStruct((block, q_cols), queries.dtype),
+        in_specs=[pl.BlockSpec(memory_space=pltpu.VMEM)] * 2,
+        out_specs=pl.BlockSpec(memory_space=pltpu.VMEM),
+        compiler_params=pltpu.CompilerParams(vmem_limit_bytes=8 * 1024 * 1024),
+    )(acc, total)
 
 
 def solution(mesh):

time: 23.5 us -> 20.3 us (0.86)
  local copies, waits for them, and re-layouts: 3.82 us -> 0 us
  Pallas kernels: 19.4 us -> 20.1 us
    unnamed x9 -> x0, local copies, waits for them, and re-layouts: 3.82 us -> none
    pallas_call x0 -> x1, Pallas kernels: none -> 0.85 us  [local(): pl.pallas_call(finish, out_shape=jax.ShapeDtypeStruct((block, q_cols), qu...]
where the time goes in v2:
time: 20.3 us; the launch traced here: 20.2 us
  Pallas kernels  20.1 us (99%)
    pallas_call x1, Pallas kernels, local(): pl.pallas_call(functools.partial(kernel, outer, inner, heads), out_shape=...  19.3 us
    pallas_call x1, Pallas kernels, local(): pl.pallas_call(finish, out_shape=jax.ShapeDtypeStruct((block, q_cols), qu...  0.85 us

profile of v2, /device:TPU:0, one launch (start us, length us, event | category | flops | bytes accessed | tf_op | source)
XLA Modules:
  0.0 20.2 jit_solution(13607048512459084775)
XLA Ops:
  0.0 19.3 %shard_map.46 = (f32[128,1024]{1,0:T(8,128)S(1)}, f32[1,1024]{1,0:T(1,128)S(1)}) custom-call(s32[8]{0:T(128)} %order.1, bf16[128,1024]{1,0:T(8,128)(2,1)} %q_hbm.1, bf16[32,512]{1,0:T(8,128)(2,1)} %k_hbm.1, bf16[32,512]{1,0:T(8,128)(2,1)} %v_hbm.1), custom_call_target="tpu_custom_call" | custom-call | tf_op jit(solution)/shard_map/pallas_call | solution.py:212
  19.3 0.8 %shard_map.47 = bf16[128,1024]{1,0:T(8,128)(2,1)} custom-call(f32[128,1024]{1,0:T(8,128)S(1)} %get-tuple-element.7.acc, f32[1,1024]{1,0:T(1,128)S(1)} %get-tuple-element.8.total), custom_call_target="tpu_custom_call" | custom-call | tf_op jit(solution)/shard_map/pallas_call | solution.py:240

commit v3 on v2

--- a/solution.py
+++ b/solution.py
@@ -17,7 +17,7 @@
     outer, inner, heads,
     order, q_hbm, k_hbm, v_hbm, acc, total,
     q_ref, k_ref, v_ref, kz, vz, kd, vd, high,
-    load_sem, zsend, zrecv, psend, precv,
+    load_sem, own_sem, zsend, zrecv, psend, precv,
 ):
     rows, _ = k_ref.shape
     block = q_ref.shape[0]
@@ -27,6 +27,8 @@
     o, j = seq // inner, lax.rem(seq, inner)
     power = outer & (outer - 1) == 0
 
+    bits = [1 << i for i in range(outer.bit_length() - 1)] if power else range(1, outer)
+
     def source(k):
         return jnp.bitwise_xor(o, k) if power else lax.rem(o - k + outer, outer)
 
@@ -50,11 +52,10 @@
         j2, h2 = member(dj, dh)
         pl.semaphore_signal(barrier, inc=1, device_id=(o * inner + j2, h2), device_id_type=MESH)
 
-    def greet(k, c):
+    for k in bits:
         pl.semaphore_signal(
             barrier, inc=1, device_id=(target(k) * inner + j, head), device_id_type=MESH
         )
-        return c
 
     def steps(first, last, body):
         if last - first <= 8:
@@ -63,30 +64,39 @@
         else:
             lax.fori_loop(first, last, body, 0)
 
-    steps(1, outer, greet)
-    pl.semaphore_wait(barrier, len(group) - 1 + outer - 1)
+    pl.semaphore_wait(barrier, len(group) - 1 + len(bits))
     loads[0].wait()
     loads[1].wait()
 
-    def zcopy(k, which):
-        own, far = ((k_ref, kz), (v_ref, vz))[which]
+    def zcopy(piece, k, bit, which):
         return pltpu.make_async_remote_copy(
-            src_ref=own,
-            dst_ref=far.at[k - 1],
+            src_ref=piece,
+            dst_ref=(kz, vz)[which].at[k - 1],
             send_sem=zsend.at[which],
             recv_sem=zrecv.at[k, which],
-            device_id=(target(k) * inner + j, head),
+            device_id=(target(bit) * inner + j, head),
             device_id_type=MESH,
         )
+
+    def forward(piece, k, which):
+        for bit in bits:
+            if isinstance(k, int):
+                if bit < k & -k:
+                    zcopy(piece, k + bit, bit, which).start()
+            else:
+
+                @pl.when(bit < (k & -k))
+                def _(bit=bit):
+                    zcopy(piece, k + bit, bit, which).start()
 
     def scatter(piece, k, which):
         dst = (kd, vd)[which]
         place = pl.ds(pl.multiple_of(j * block + head * rows, rows), rows)
-        for dj, dh in group:
+        for dj, dh in group[::-1]:
             j2, h2 = member(dj, dh)
             src = piece.at[:, pl.ds(pl.multiple_of(h2 * width, width), width)]
             if dj == 0 and dh == 0:
-                pltpu.make_async_copy(src, dst.at[k, place], load_sem.at[3 + which]).start()
+                pltpu.make_async_copy(src, dst.at[k, place], own_sem.at[k, which]).start()
             else:
                 pltpu.make_async_remote_copy(
                     src_ref=src,
@@ -96,19 +106,22 @@
                     device_id=(o * inner + j2, h2),
                     device_id_type=MESH,
                 ).start()
-        src = piece.at[:, pl.ds(pl.multiple_of(head * width, width), width)]
-        pltpu.make_async_copy(src, dst.at[k, place], load_sem.at[3 + which]).wait()
 
     others = pl.ds(0, (len(group) - 1) * rows)
 
     def landed(k, which):
         dst = (kd, vd)[which].at[k, others]
         pltpu.make_async_copy(dst, dst, precv.at[k, which]).wait()
+        dst = (kd, vd)[which].at[k, pl.ds(0, rows)]
+        pltpu.make_async_copy(dst, dst, own_sem.at[k, which]).wait()
 
     def relay(k, c=0):
         for which in range(2):
-            zcopy(k, which).wait_recv()
-            scatter((kz, vz)[which].at[k - 1], k, which)
+            piece = (kz, vz)[which].at[k - 1]
+            zcopy(piece, k, bits[0], which).wait_recv()
+            if power:
+                forward(piece, k, which)
+            scatter(piece, k, which)
         return c
 
     mine = order[seq]
@@ -160,22 +173,30 @@
                 total[:, at] = total[:, at] * scale + t
                 acc[:, at] = acc[:, at] * scale + pv
 
+    for bit in bits[::-1]:
+        for which in range(2):
+            zcopy((k_ref, v_ref)[which], bit, bit, which).start()
     for which in range(2):
-        steps(1, outer, lambda k, c, which=which: (zcopy(k, which).start(), c)[1])
         scatter((k_ref, v_ref)[which], 0, which)
     loads[2].wait()
-    if outer > 1:
-        relay(1)
-    absorb(0, True)
-
-    def later(k, c):
-        relay(k + 1)
-        absorb(k, False)
-        return c
-
-    steps(1, outer - 1, later)
-    if outer > 1:
-        absorb(outer - 1, False)
+    if outer <= 8:
+        turn = sorted(range(outer), key=lambda k: [k >> i & 1 for i in range(outer)])
+        ahead = min(2, outer - 1)
+        for k in turn[1 : ahead + 1]:
+            relay(k)
+        for i, k in enumerate(turn):
+            if 0 < i and i + ahead < outer:
+                relay(turn[i + ahead])
+            absorb(k, i == 0)
+    else:
+        absorb(0, True)
+
+        def later(k, c):
+            relay(k)
+            absorb(k, False)
+            return c
+
+        lax.fori_loop(1, outer, later, 0)
 
     if outer > 1:
         for which in range(2):
@@ -227,7 +248,8 @@
             pltpu.VMEM((outer, inner * block, width), bf16),
             pltpu.VMEM((outer, inner * block, width), bf16),
             pltpu.VMEM((1, lanes), f32),
-            pltpu.SemaphoreType.DMA((5,)),
+            pltpu.SemaphoreType.DMA((3,)),
+            pltpu.SemaphoreType.DMA((outer, 2)),
             pltpu.SemaphoreType.DMA((2,)),
             pltpu.SemaphoreType.DMA((outer, 2)),
             pltpu.SemaphoreType.DMA((outer, 2)),

time: 20.3 us -> 19.1 us (0.941)
  Pallas kernels: 20.1 us -> 18.9 us
    pallas_call x1, Pallas kernels: 19.3 us -> 18.1 us  [local(): pl.pallas_call(functools.partial(kernel, outer, inner, heads), out_shape=...]
where the time goes in v3:
time: 19.1 us; the launch traced here: 18.9 us
  Pallas kernels  18.9 us (99%)
    pallas_call x1, Pallas kernels, local(): pl.pallas_call(functools.partial(kernel, outer, inner, heads), out_shape=...  18.1 us
    pallas_call x1, Pallas kernels, local(): pl.pallas_call(finish, out_shape=jax.ShapeDtypeStruct((block, q_cols), qu...  0.85 us

profile of v3, /device:TPU:0, one launch (start us, length us, event | category | flops | bytes accessed | tf_op | source)
XLA Modules:
  0.0 18.9 jit_solution(14624667525030326189)
XLA Ops:
  0.0 18.1 %shard_map.46 = (f32[128,1024]{1,0:T(8,128)S(1)}, f32[1,1024]{1,0:T(1,128)S(1)}) custom-call(s32[8]{0:T(128)} %order.1, bf16[128,1024]{1,0:T(8,128)(2,1)} %q_hbm.1, bf16[32,512]{1,0:T(8,128)(2,1)} %k_hbm.1, bf16[32,512]{1,0:T(8,128)(2,1)} %v_hbm.1), custom_call_target="tpu_custom_call" | custom-call | tf_op jit(solution)/shard_map/pallas_call | solution.py:233
  18.1 0.8 %shard_map.47 = bf16[128,1024]{1,0:T(8,128)(2,1)} custom-call(f32[128,1024]{1,0:T(8,128)S(1)} %get-tuple-element.7.acc, f32[1,1024]{1,0:T(1,128)S(1)} %get-tuple-element.8.total), custom_call_target="tpu_custom_call" | custom-call | tf_op jit(solution)/shard_map/pallas_call | solution.py:262
